TPU v7x, 32 devices: a whole 2x2x4 slice. The times are simulated.
32 devices in a mesh: row: 16 (over z, y, core), col: 2 (over x).
Axes of the slice: x: 2, y: 2, z: 4, core: 2. Of those that a mesh axis runs over, the one named last changes fastest.
Arguments:
- vectors: float32 [1024, 32768], P(('row', 'col')), may hold values from -6 to 6
- reflectors: float32 [6, 128, 32768], P(None, 'col', 'row')
- factors: float32 [6, 128, 128], replicated, as said below
Outputs:
- transformed: float32 [1024, 32768], P('col', 'row')
Inputs may be any that keep to these rules, and one draw needn't show every extreme that they name: factors[k] is upper triangular, and its inverse equals the strict upper part of reflectors[k] reflectors[k]^T plus half of that product's diagonal, so each panel is orthogonal.
All inputs are finite; a program needn't handle non-finite values.
Results may differ from a plain program's by a relative error of at most 0.0001.
Values sent between devices are 32-bit elements; how exact they have to be, the bound alone decides.
A program may use at most 128 MiB of HBM per device.

v0:
```python
import functools

import jax
import jax.numpy as jnp
from jax import lax
from jax.experimental import pallas as pl
from jax.experimental.pallas import tpu as pltpu
from jax.sharding import PartitionSpec as P

MESH = pl.DeviceIdType.MESH
HIGH = lax.Precision.HIGH


def nt(left, right, precision):
    return lax.dot_general(
        left,
        right,
        (((1,), (1,)), ((), ())),
        precision=precision,
        preferred_element_type=jnp.float32,
    )


def split(value):
    top = value.astype(jnp.bfloat16)
    return top, (value - top.astype(jnp.float32)).astype(jnp.bfloat16)


def plain_nt(left, right):
    return lax.dot_general(
        left, right, (((1,), (1,)), ((), ())), preferred_element_type=jnp.float32
    )


def strides_of(rows):
    found = []
    stride = 1
    while stride < rows:
        found.append(stride)
        stride *= 2
    return found


def orders_of(rows):
    base = strides_of(rows)
    return [base, base[:1] + base[2:] + base[1:2]]


class Reduce:
    def __init__(self, row, row_count, source, landing, out, sems):
        self.row = row
        self.source = source
        self.landing = landing
        self.out = out
        self.sems = sems
        total = source.shape[0]
        self.orders = orders_of(row_count)
        self.part = total // len(self.orders)
        self.previous = [source.at[pl.ds(i * self.part, self.part)] for i in range(2)]
        self.offset = [i * self.part for i in range(2)]
        self.count = len(self.orders[0])
        self.pending = None

    def bit(self, stride):
        return lax.rem(self.row // stride, 2)

    def partner(self, stride):
        return self.row + stride * (1 - 2 * self.bit(stride))

    def copy(self, source, target, number, stride):
        return pltpu.make_async_remote_copy(
            src_ref=source,
            dst_ref=target,
            send_sem=self.sems.at[0, number],
            recv_sem=self.sems.at[1, number],
            device_id={"row": self.partner(stride)},
            device_id_type=MESH,
        )

    def halve_start(self, stage):
        self.pending = []
        half = self.part >> (stage + 1)
        start = self.part - (self.part >> stage)
        for i in range(2):
            stride = self.orders[i][stage]
            bit = self.bit(stride)
            away = pl.ds(pl.multiple_of((1 - bit) * half, 8), half)
            here = self.landing.at[i, pl.ds(start, half)]
            item = self.copy(self.previous[i].at[away], here, stage * 2 + i, stride)
            item.start()
            self.pending.append((item, here, bit, half))

    def halve_end(self):
        for i in range(2):
            item, here, bit, half = self.pending[i]
            item.wait()
            keep = pl.ds(pl.multiple_of(bit * half, 8), half)
            here[...] = here[...] + self.previous[i][keep, :]
            self.previous[i] = here
            self.offset[i] = self.offset[i] + bit * half

    def place(self, i, value):
        size = value.shape[0]
        self.out[pl.ds(pl.multiple_of(self.offset[i], 8), size), :] = value

    def double_start(self, stage):
        self.pending = []
        size = self.part >> (self.count - stage)
        for i in range(2):
            stride = self.orders[i][self.count - 1 - stage]
            where = self.out.at[pl.ds(pl.multiple_of(self.offset[i], 8), size)]
            item = self.copy(where, where, (self.count + stage) * 2 + i, stride)
            item.start()
            self.pending.append((item, self.bit(stride) * size))

    def double_end(self):
        for i in range(2):
            item, back = self.pending[i]
            item.wait()
            self.offset[i] = self.offset[i] - back


def exchange_kernel(
    row_count, col_count, vectors, reflectors, current, panels, gram,
    stage, held, tops, lows, partial, landing,
    row_sems, far_sems, gather_sems, local_sems, gram_sems,
):
    row = lax.axis_index("row")
    col = lax.axis_index("col")
    local = vectors.shape[0]
    length = current.shape[1]
    count, part, _ = reflectors.shape
    width = part * col_count

    barrier = pltpu.get_barrier_semaphore()
    for step in range(1, row_count):
        pl.semaphore_signal(
            barrier, inc=1, device_id={"row": lax.rem(row + step, row_count)}, device_id_type=MESH
        )
    for step in range(1, col_count):
        pl.semaphore_signal(
            barrier, inc=1, device_id={"col": lax.rem(col + step, col_count)}, device_id_type=MESH
        )
    pl.semaphore_wait(barrier, row_count + col_count - 2)

    def slot_rows(slot):
        return pl.ds(pl.multiple_of(slot * local, 8), local)

    gathers = []
    for step in range(1, col_count):
        for panel in range(count):
            number = (step - 1) * count + panel
            item = pltpu.make_async_remote_copy(
                src_ref=reflectors.at[panel],
                dst_ref=held.at[pl.ds(pl.multiple_of(panel * width + col * part, 8), part)],
                send_sem=gather_sems.at[0, number],
                recv_sem=gather_sems.at[1, number],
                device_id={"col": lax.rem(col + step, col_count)},
                device_id_type=MESH,
            )
            item.start()
            gathers.append(item)

    middle = row_count // 2
    steps = sorted(range(1, row_count), key=lambda step: (abs(step - middle), step))
    mine = row * col_count + col
    my_target = mine // row_count
    my_slot = lax.rem(mine, row_count)
    sends = {}
    for step in steps:
        other = lax.rem(row + step, row_count)
        source = vectors.at[:, pl.ds(pl.multiple_of(other * length, 128), length)]

        def sending(target, source=source, step=step, other=other):
            return pltpu.make_async_remote_copy(
                src_ref=source,
                dst_ref=target,
                send_sem=row_sems.at[0, step],
                recv_sem=row_sems.at[1, step],
                device_id={"row": other},
                device_id_type=MESH,
            )

        @pl.when(my_target == col)
        def _():
            sending(current.at[slot_rows(my_slot)]).start()

        @pl.when(my_target != col)
        def _():
            sending(stage.at[row]).start()

        sends[step] = sending(stage.at[row])

    own = pltpu.make_async_copy(
        vectors.at[:, pl.ds(pl.multiple_of(row * length, 128), length)], stage.at[row], local_sems.at[0]
    )
    own.start()
    own_panels = []
    for panel in range(count):
        item = pltpu.make_async_copy(
            reflectors.at[panel],
            held.at[pl.ds(pl.multiple_of(panel * width + col * part, 8), part)],
            local_sems.at[1 + panel],
        )
        item.start()
        own_panels.append(item)

    def onward(source_row):
        block = source_row * col_count + col
        target = block // row_count
        slot = lax.rem(block, row_count)
        return target, pltpu.make_async_remote_copy(
            src_ref=stage.at[source_row],
            dst_ref=current.at[slot_rows(slot)],
            send_sem=far_sems.at[0, slot],
            recv_sem=far_sems.at[1, slot],
            device_id={"col": target},
            device_id_type=MESH,
        )

    own.wait()
    own_target, own_far = onward(row)
    own_here = pltpu.make_async_copy(stage.at[row], current.at[slot_rows(my_slot)], local_sems.at[0])

    @pl.when(own_target == col)
    def _():
        own_here.start()
        own_here.wait()

    @pl.when(own_target != col)
    def _():
        own_far.start()

    def arrive(step):
        source_row = lax.rem(row - step + row_count, row_count)
        target, far = onward(source_row)
        sends[step].wait_recv()

        @pl.when(target != col)
        def _():
            far.start()

    early = (len(steps) + 1) // 2
    for step in steps[:early]:
        arrive(step)
    for item in own_panels:
        item.wait()
    for item in gathers:
        item.wait()
    keep_panels = pltpu.make_async_copy(held, panels, local_sems.at[0])
    keep_panels.start()

    def split_rows(i, carry):
        rows = pl.ds(pl.multiple_of(i * 32, 32), 32)
        top, low = split(held[rows, :])
        tops[rows, :] = top
        lows[rows, :] = low
        return carry

    lax.fori_loop(0, count * width // 32, split_rows, 0)
    base = 0
    for panel in range(count - 1):
        right = pl.ds(panel * width, width)

        def block(i, carry, right=right, base=base, panel=panel):
            left = pl.ds(pl.multiple_of((panel + 1 + i) * width, 128), width)
            value = plain_nt(tops[left, :], tops[right, :])
            value = value + plain_nt(tops[left, :], lows[right, :])
            value = value + plain_nt(lows[left, :], tops[right, :])
            partial[pl.ds(pl.multiple_of(base + i * width, 128), width), :] = value
            return carry

        lax.fori_loop(0, count - 1 - panel, block, 0)
        base += (count - 1 - panel) * width
    partial[pl.ds(base, partial.shape[0] - base), :] = jnp.zeros(
        (partial.shape[0] - base, width), jnp.float32
    )

    late = list(steps[early:])
    reduce = Reduce(row, row_count, partial, landing, gram, gram_sems)
    rounds = 2 * reduce.count
    done = 0
    for number in range(rounds):
        if number < reduce.count:
            reduce.halve_start(number)
        else:
            if number == reduce.count:
                for i in range(2):
                    reduce.place(i, reduce.previous[i][...])
            reduce.double_start(number - reduce.count)
        goal = len(late) * (number + 1) // rounds
        for step in late[done:goal]:
            arrive(step)
        done = goal
        if number < reduce.count:
            reduce.halve_end()
        else:
            reduce.double_end()

    keep_panels.wait()
    for step in steps:
        sends[step].wait_send()
    for source_row in range(row_count):
        target, far = onward(source_row)

        @pl.when(target != col)
        def _():
            far.wait_send()

    for slot in range(row_count):
        far = pltpu.make_async_remote_copy(
            src_ref=stage.at[0],
            dst_ref=current.at[slot_rows(slot)],
            send_sem=far_sems.at[0, slot],
            recv_sem=far_sems.at[1, slot],
            device_id={"col": col},
            device_id_type=MESH,
        )

        @pl.when(lax.rem(col * row_count + slot, col_count) != col)
        def _():
            far.wait_recv()


def solve_kernel(row_count, projection, gram, factors, update, landing, sems):
    row = lax.axis_index("row")
    barrier = pltpu.get_barrier_semaphore()
    for stride in strides_of(row_count):
        other = row + stride * (1 - 2 * lax.rem(row // stride, 2))
        pl.semaphore_signal(barrier, inc=1, device_id={"row": other}, device_id_type=MESH)
    pl.semaphore_wait(barrier, len(strides_of(row_count)))
    count, width, _ = factors.shape
    reduce = Reduce(row, row_count, projection, landing, update, sems)
    for stage in range(reduce.count):
        reduce.halve_start(stage)
        reduce.halve_end()
    value = jnp.concatenate([reduce.previous[i][...] for i in range(2)], axis=0)
    starts = []
    base = 0
    for panel in range(count):
        starts.append(base)
        base += (count - 1 - panel) * width
    solved = None
    for panel in range(count - 1, -1, -1):
        term = value[:, panel * width : (panel + 1) * width]
        if solved is not None:
            rows = (count - 1 - panel) * width
            term = term - jnp.dot(
                solved,
                gram[pl.ds(starts[panel], rows), :],
                precision=lax.Precision.HIGHEST,
                preferred_element_type=jnp.float32,
            )
        piece = nt(term, factors[panel], lax.Precision.HIGHEST)
        solved = piece if solved is None else jnp.concatenate([piece, solved], axis=1)
    size = value.shape[0] // 2
    for i in range(2):
        reduce.place(i, solved[i * size : (i + 1) * size, :])
    for stage in range(reduce.count):
        reduce.double_start(stage)
        reduce.double_end()


def on_device(vectors, reflectors, factors):
    local_count, total_length = vectors.shape
    row_count = lax.axis_size("row")
    col_count = lax.axis_size("col")
    length = total_length // row_count
    count, part, _ = reflectors.shape
    width = part * col_count
    rows = local_count * row_count
    stages = len(strides_of(row_count))
    unit = 16 * row_count
    gram_rows = -(-(count * (count - 1) // 2 * width) // unit) * unit
    anywhere = pl.BlockSpec(memory_space=pl.ANY)
    vmem = pl.BlockSpec(memory_space=pltpu.VMEM)
    dma = pltpu.SemaphoreType.DMA
    current, panels, gram = pl.pallas_call(
        functools.partial(exchange_kernel, row_count, col_count),
        name="exchange",
        out_shape=(
            jax.ShapeDtypeStruct((rows, length), jnp.float32),
            jax.ShapeDtypeStruct((count * width, length), jnp.float32),
            jax.ShapeDtypeStruct((gram_rows, width), jnp.float32),
        ),
        in_specs=[anywhere, anywhere],
        out_specs=(anywhere, anywhere, vmem),
        scratch_shapes=[
            pltpu.VMEM((row_count, local_count, length), jnp.float32),
            pltpu.VMEM((count * width, length), jnp.float32),
            pltpu.VMEM((count * width, length), jnp.bfloat16),
            pltpu.VMEM((count * width, length), jnp.bfloat16),
            pltpu.VMEM((gram_rows, width), jnp.float32),
            pltpu.VMEM((2, gram_rows // 2, width), jnp.float32),
            dma((2, row_count)),
            dma((2, row_count)),
            dma((2, (col_count - 1) * count)),
            dma((1 + count,)),
            dma((2, 4 * stages)),
        ],
        compiler_params=pltpu.CompilerParams(
            collective_id=0, has_side_effects=True, vmem_limit_bytes=48 * 1024 * 1024
        ),
    )(vectors, reflectors)
    projection = nt(current, panels, HIGH)
    update = pl.pallas_call(
        functools.partial(solve_kernel, row_count),
        name="solve",
        out_shape=jax.ShapeDtypeStruct((rows, count * width), jnp.float32),
        in_specs=[vmem, vmem, vmem],
        out_specs=vmem,
        scratch_shapes=[
            pltpu.VMEM((2, rows // 2, count * width), jnp.float32),
            dma((2, 4 * stages)),
        ],
        compiler_params=pltpu.CompilerParams(
            collective_id=1, has_side_effects=True, vmem_limit_bytes=32 * 1024 * 1024
        ),
    )(projection, gram, factors)
    return current - jnp.dot(update, panels, precision=HIGH, preferred_element_type=jnp.float32)


def solution(mesh):
    return jax.shard_map(
        on_device,
        mesh=mesh,
        in_specs=(P(("row", "col"), None), P(None, "col", "row"), P()),
        out_specs=P("col", "row"),
        check_vma=False,
    )
```

profile of v0, /device:TPU:0, one launch (start us, length us, event | category | flops | bytes accessed | tf_op | source)
XLA Modules:
  0.0 206.8 jit_solution(15149009957420439224)
XLA Ops:
  0.0 0.0 copy-start
  0.0 1.9 copy-done
  1.9 139.9 %exchange.1 = (f32[512,2048]{1,0:T(8,128)}, f32[768,2048]{1,0:T(8,128)}, f32[2048,128]{1,0:T(8,128)S(1)}) custom-call(f32[32,32768]{1,0:T(8,128)} %vectors.1, f32[6,64,2048]{2,1,0:T(8,128)S(1)} %copy-done), custom_call_target="tpu_custom_call" | custom-call | tf_op jit(solution)/shard_map/exchange/pallas_call | solution.py:378
  141.8 0.0 copy-start.1
  141.8 0.0 copy-start.2
  141.8 9.3 %fusion.projection = f32[512,768]{1,0:T(8,128)S(1)} fusion(f32[512,2048]{1,0:T(8,128)} %get-tuple-element.8, f32[768,2048]{1,0:T(8,128)} %get-tuple-element.9), kind=kOutput, calls=%fused_computation.1 | convolution fusion | flops 4831838208 | bytes 12058624 | tf_op jit(solution)/shard_map/dot_general | solution.py:15
  151.1 0.0 copy-done.1
  151.1 0.0 copy-start.3
  151.1 48.9 %solve.1 = f32[512,768]{1,0:T(8,128)S(1)} custom-call(f32[512,768]{1,0:T(8,128)S(1)} %fusion.projection, f32[2048,128]{1,0:T(8,128)S(1)} %get-tuple-element.10.gram, f32[6,128,128]{2,1,0:T(8,128)S(1)} %copy-done.1), custom_call_target="tpu_custom_call" | custom-call | tf_op jit(solution)/shard_map/solve/pallas_call | solution.py:406
  200.0 0.0 copy-done.2
  200.0 0.0 copy-done.3
  200.0 6.7 %convolution_subtract_fusion = f32[512,2048]{1,0:T(8,128)} fusion(f32[512,2048]{1,0:T(8,128)S(1)} %copy-done.3, f32[512,768]{1,0:T(8,128)S(1)} %solve.1, f32[768,2048]{1,0:T(8,128)S(1)} %copy-done.2), kind=kOutput, calls=%fused_computation | convolution fusion | flops 4832886784 | bytes 16252928 | tf_op jit(solution)/shard_map/dot_general | solution.py:420
Async XLA Ops:
  0.0 1.9 copy-start
  141.8 9.3 %copy-start.1 = (f32[6,128,128]{2,1,0:T(8,128)S(1)}, f32[6,128,128]{2,1,0:T(8,128)}, u32[]{:S(2)}) copy-start(f32[6,128,128]{2,1,0:T(8,128)} %factors.1) | copy-start | bytes 1179652
  141.8 58.2 %copy-start.2 = (f32[768,2048]{1,0:T(8,128)S(1)}, f32[768,2048]{1,0:T(8,128)}, u32[]{:S(2)}) copy-start(f32[768,2048]{1,0:T(8,128)} %get-tuple-element.9) | copy-start | bytes 18874372
  151.1 48.9 %copy-start.3 = (f32[512,2048]{1,0:T(8,128)S(1)}, f32[512,2048]{1,0:T(8,128)}, u32[]{:S(2)}) copy-start(f32[512,2048]{1,0:T(8,128)} %get-tuple-element.8) | copy-start | bytes 12582916
where the time goes:
time: 207 us
  Pallas kernels  189 us (91%)
  matrix products  16 us (8%)
    pallas_call x1, Pallas kernels, on_device(): pl.pallas_call(functools.partial(exchange_kernel, row_count, col_count),...  140 us
    pallas_call x1, Pallas kernels, on_device(): pl.pallas_call(functools.partial(solve_kernel, row_count), name='solve',...  48.9 us
    dot_general x1, matrix products, nt(): lax.dot_general(left, right, (((1,), (1,)), ((), ())), precision=precisio...  9.25 us
    dot_general x1, matrix products, on_device(): jnp.dot(update, panels, precision=HIGH, preferred_element_type=jnp.float32)  6.73 us

commit v1 on v0

--- a/solution.py
+++ b/solution.py
@@ -120,10 +120,11 @@
             self.offset[i] = self.offset[i] - back
 
 
-def exchange_kernel(
-    row_count, col_count, vectors, reflectors, current, panels, gram,
-    stage, held, tops, lows, partial, landing,
-    row_sems, far_sems, gather_sems, local_sems, gram_sems,
+def kernel(
+    row_count, col_count, vectors, reflectors, factors, current, panels, update,
+    stage, held, tops, lows, here, here_top, here_low, projection, solved_rows,
+    landing, partial, gram, gram_landing,
+    row_sems, far_sems, gather_sems, local_sems, out_sems, gram_sems, first_sems, second_sems,
 ):
     row = lax.axis_index("row")
     col = lax.axis_index("col")
@@ -131,6 +132,9 @@
     length = current.shape[1]
     count, part, _ = reflectors.shape
     width = part * col_count
+    group = row_count // col_count
+    half_slots = row_count // 2
+    half_rows = half_slots * local
 
     barrier = pltpu.get_barrier_semaphore()
     for step in range(1, row_count):
@@ -161,11 +165,16 @@
             item.start()
             gathers.append(item)
 
+    def onward(source_row):
+        block = source_row * col_count + col
+        target = block // row_count
+        slot = lax.rem(block, row_count)
+        place = lax.rem(slot - target + col_count, col_count) * group + slot // col_count
+        return target, place
+
     middle = row_count // 2
     steps = sorted(range(1, row_count), key=lambda step: (abs(step - middle), step))
-    mine = row * col_count + col
-    my_target = mine // row_count
-    my_slot = lax.rem(mine, row_count)
+    my_target, my_place = onward(row)
     sends = {}
     for step in steps:
         other = lax.rem(row + step, row_count)
@@ -183,7 +192,7 @@
 
         @pl.when(my_target == col)
         def _():
-            sending(current.at[slot_rows(my_slot)]).start()
+            sending(here.at[slot_rows(my_place)]).start()
 
         @pl.when(my_target != col)
         def _():
@@ -205,22 +214,20 @@
         item.start()
         own_panels.append(item)
 
-    def onward(source_row):
-        block = source_row * col_count + col
-        target = block // row_count
-        slot = lax.rem(block, row_count)
+    def far_copy(source_row):
+        target, place = onward(source_row)
         return target, pltpu.make_async_remote_copy(
             src_ref=stage.at[source_row],
-            dst_ref=current.at[slot_rows(slot)],
-            send_sem=far_sems.at[0, slot],
-            recv_sem=far_sems.at[1, slot],
+            dst_ref=here.at[slot_rows(place)],
+            send_sem=far_sems.at[0, place],
+            recv_sem=far_sems.at[1, place],
             device_id={"col": target},
             device_id_type=MESH,
         )
 
     own.wait()
-    own_target, own_far = onward(row)
-    own_here = pltpu.make_async_copy(stage.at[row], current.at[slot_rows(my_slot)], local_sems.at[0])
+    own_target, own_far = far_copy(row)
+    own_here = pltpu.make_async_copy(stage.at[row], here.at[slot_rows(my_place)], local_sems.at[0])
 
     @pl.when(own_target == col)
     def _():
@@ -232,8 +239,7 @@
         own_far.start()
 
     def arrive(step):
-        source_row = lax.rem(row - step + row_count, row_count)
-        target, far = onward(source_row)
+        target, far = far_copy(lax.rem(row - step + row_count, row_count))
         sends[step].wait_recv()
 
         @pl.when(target != col)
@@ -259,7 +265,9 @@
 
     lax.fori_loop(0, count * width // 32, split_rows, 0)
     base = 0
-    for panel in range(count - 1):
+    starts = []
+    for panel in range(count):
+        starts.append(base)
         right = pl.ds(panel * width, width)
 
         def block(i, carry, right=right, base=base, panel=panel):
@@ -270,95 +278,136 @@
             partial[pl.ds(pl.multiple_of(base + i * width, 128), width), :] = value
             return carry
 
-        lax.fori_loop(0, count - 1 - panel, block, 0)
+        if panel < count - 1:
+            lax.fori_loop(0, count - 1 - panel, block, 0)
         base += (count - 1 - panel) * width
     partial[pl.ds(base, partial.shape[0] - base), :] = jnp.zeros(
         (partial.shape[0] - base, width), jnp.float32
     )
 
+    def put_out(source, target, place, which):
+        slot = (place % group) * col_count + lax.rem(col + place // group, col_count)
+        item = pltpu.make_async_copy(
+            source.at[slot_rows(place)], target.at[slot_rows(slot)], out_sems.at[which, place]
+        )
+        item.start()
+        return item
+
+    outs = []
+    tile = 2 * width if count % 2 == 0 else width
+
+    def project(chunk):
+        for place in range(chunk * half_slots, (chunk + 1) * half_slots):
+            if place >= group:
+                pltpu.make_async_remote_copy(
+                    src_ref=stage.at[0],
+                    dst_ref=here.at[slot_rows(place)],
+                    send_sem=far_sems.at[0, place],
+                    recv_sem=far_sems.at[1, place],
+                    device_id={"col": col},
+                    device_id_type=MESH,
+                ).wait_recv()
+            outs.append(put_out(here, current, place, 0))
+
+        def split_here(i, carry):
+            rows = pl.ds(pl.multiple_of(i * 32, 32), 32)
+            top, low = split(here[pl.ds(pl.multiple_of(chunk * half_rows + i * 32, 32), 32), :])
+            here_top[rows, :] = top
+            here_low[rows, :] = low
+            return carry
+
+        lax.fori_loop(0, half_rows // 32, split_here, 0)
+
+        def columns(i, carry):
+            right = pl.ds(pl.multiple_of(i * tile, 128), tile)
+            value = plain_nt(here_top[...], tops[right, :])
+            value = value + plain_nt(here_top[...], lows[right, :])
+            value = value + plain_nt(here_low[...], tops[right, :])
+            projection[pl.ds(chunk * half_rows, half_rows), right] = value
+            return carry
+
+        lax.fori_loop(0, count * width // tile, columns, 0)
+
+    def solve(reduce):
+        value = jnp.concatenate([reduce.previous[i][...] for i in range(2)], axis=0)
+        solved = None
+        for panel in range(count - 1, -1, -1):
+            term = value[:, panel * width : (panel + 1) * width]
+            if solved is not None:
+                rows = (count - 1 - panel) * width
+                term = term - jnp.dot(
+                    solved,
+                    gram[pl.ds(starts[panel], rows), :],
+                    precision=lax.Precision.HIGHEST,
+                    preferred_element_type=jnp.float32,
+                )
+            piece = nt(term, factors[panel], lax.Precision.HIGHEST)
+            solved = piece if solved is None else jnp.concatenate([piece, solved], axis=1)
+        size = value.shape[0] // 2
+        for i in range(2):
+            reduce.place(i, solved[i * size : (i + 1) * size, :])
+
+    def chunk_reduce(chunk, sems):
+        rows = pl.ds(chunk * half_rows, half_rows)
+        return Reduce(
+            row, row_count, projection.at[rows], landing.at[chunk], solved_rows.at[rows], sems
+        )
+
     late = list(steps[early:])
-    reduce = Reduce(row, row_count, partial, landing, gram, gram_sems)
-    rounds = 2 * reduce.count
+    inner = Reduce(row, row_count, partial, gram_landing, gram, gram_sems)
+    stages = inner.count
     done = 0
-    for number in range(rounds):
-        if number < reduce.count:
-            reduce.halve_start(number)
-        else:
-            if number == reduce.count:
-                for i in range(2):
-                    reduce.place(i, reduce.previous[i][...])
-            reduce.double_start(number - reduce.count)
-        goal = len(late) * (number + 1) // rounds
+    for number in range(stages):
+        inner.halve_start(number)
+        goal = len(late) * (number + 1) // stages
         for step in late[done:goal]:
             arrive(step)
         done = goal
-        if number < reduce.count:
-            reduce.halve_end()
-        else:
-            reduce.double_end()
+        inner.halve_end()
+    for i in range(2):
+        inner.place(i, inner.previous[i][...])
+    inner.double_start(0)
+    project(0)
+    inner.double_end()
+    first = chunk_reduce(0, first_sems)
+    for number in range(stages):
+        first.halve_start(number)
+        if number + 1 < stages:
+            inner.double_start(number + 1)
+            inner.double_end()
+        first.halve_end()
+    solve(first)
+    first.double_start(0)
+    project(1)
+    first.double_end()
+    second = chunk_reduce(1, second_sems)
+    for number in range(stages):
+        second.halve_start(number)
+        if number + 1 < stages:
+            first.double_start(number + 1)
+            first.double_end()
+        second.halve_end()
+    for place in range(half_slots):
+        outs.append(put_out(solved_rows, update, place, 1))
+    solve(second)
+    for number in range(stages):
+        second.double_start(number)
+        second.double_end()
+    for place in range(half_slots, row_count):
+        outs.append(put_out(solved_rows, update, place, 1))
 
     keep_panels.wait()
     for step in steps:
         sends[step].wait_send()
     for source_row in range(row_count):
-        target, far = onward(source_row)
+        target, far = far_copy(source_row)
 
         @pl.when(target != col)
         def _():
             far.wait_send()
 
-    for slot in range(row_count):
-        far = pltpu.make_async_remote_copy(
-            src_ref=stage.at[0],
-            dst_ref=current.at[slot_rows(slot)],
-            send_sem=far_sems.at[0, slot],
-            recv_sem=far_sems.at[1, slot],
-            device_id={"col": col},
-            device_id_type=MESH,
-        )
-
-        @pl.when(lax.rem(col * row_count + slot, col_count) != col)
-        def _():
-            far.wait_recv()
-
-
-def solve_kernel(row_count, projection, gram, factors, update, landing, sems):
-    row = lax.axis_index("row")
-    barrier = pltpu.get_barrier_semaphore()
-    for stride in strides_of(row_count):
-        other = row + stride * (1 - 2 * lax.rem(row // stride, 2))
-        pl.semaphore_signal(barrier, inc=1, device_id={"row": other}, device_id_type=MESH)
-    pl.semaphore_wait(barrier, len(strides_of(row_count)))
-    count, width, _ = factors.shape
-    reduce = Reduce(row, row_count, projection, landing, update, sems)
-    for stage in range(reduce.count):
-        reduce.halve_start(stage)
-        reduce.halve_end()
-    value = jnp.concatenate([reduce.previous[i][...] for i in range(2)], axis=0)
-    starts = []
-    base = 0
-    for panel in range(count):
-        starts.append(base)
-        base += (count - 1 - panel) * width
-    solved = None
-    for panel in range(count - 1, -1, -1):
-        term = value[:, panel * width : (panel + 1) * width]
-        if solved is not None:
-            rows = (count - 1 - panel) * width
-            term = term - jnp.dot(
-                solved,
-                gram[pl.ds(starts[panel], rows), :],
-                precision=lax.Precision.HIGHEST,
-                preferred_element_type=jnp.float32,
-            )
-        piece = nt(term, factors[panel], lax.Precision.HIGHEST)
-        solved = piece if solved is None else jnp.concatenate([piece, solved], axis=1)
-    size = value.shape[0] // 2
-    for i in range(2):
-        reduce.place(i, solved[i * size : (i + 1) * size, :])
-    for stage in range(reduce.count):
-        reduce.double_start(stage)
-        reduce.double_end()
+    for item in outs:
+        item.wait()
 
 
 def on_device(vectors, reflectors, factors):
@@ -375,49 +424,45 @@
     anywhere = pl.BlockSpec(memory_space=pl.ANY)
     vmem = pl.BlockSpec(memory_space=pltpu.VMEM)
     dma = pltpu.SemaphoreType.DMA
-    current, panels, gram = pl.pallas_call(
-        functools.partial(exchange_kernel, row_count, col_count),
+    single, half = jnp.float32, jnp.bfloat16
+    current, panels, update = pl.pallas_call(
+        functools.partial(kernel, row_count, col_count),
         name="exchange",
         out_shape=(
-            jax.ShapeDtypeStruct((rows, length), jnp.float32),
-            jax.ShapeDtypeStruct((count * width, length), jnp.float32),
-            jax.ShapeDtypeStruct((gram_rows, width), jnp.float32),
+            jax.ShapeDtypeStruct((rows, length), single),
+            jax.ShapeDtypeStruct((count * width, length), single),
+            jax.ShapeDtypeStruct((rows, count * width), single),
         ),
-        in_specs=[anywhere, anywhere],
-        out_specs=(anywhere, anywhere, vmem),
+        in_specs=[anywhere, anywhere, vmem],
+        out_specs=(anywhere, anywhere, anywhere),
         scratch_shapes=[
-            pltpu.VMEM((row_count, local_count, length), jnp.float32),
-            pltpu.VMEM((count * width, length), jnp.float32),
-            pltpu.VMEM((count * width, length), jnp.bfloat16),
-            pltpu.VMEM((count * width, length), jnp.bfloat16),
-            pltpu.VMEM((gram_rows, width), jnp.float32),
-            pltpu.VMEM((2, gram_rows // 2, width), jnp.float32),
+            pltpu.VMEM((row_count, local_count, length), single),
+            pltpu.VMEM((count * width, length), single),
+            pltpu.VMEM((count * width, length), half),
+            pltpu.VMEM((count * width, length), half),
+            pltpu.VMEM((rows, length), single),
+            pltpu.VMEM((rows // 2, length), half),
+            pltpu.VMEM((rows // 2, length), half),
+            pltpu.VMEM((rows, count * width), single),
+            pltpu.VMEM((rows, count * width), single),
+            pltpu.VMEM((2, 2, rows // 4, count * width), single),
+            pltpu.VMEM((gram_rows, width), single),
+            pltpu.VMEM((gram_rows, width), single),
+            pltpu.VMEM((2, gram_rows // 2, width), single),
             dma((2, row_count)),
             dma((2, row_count)),
             dma((2, (col_count - 1) * count)),
             dma((1 + count,)),
+            dma((2, row_count)),
+            dma((2, 4 * stages)),
+            dma((2, 4 * stages)),
             dma((2, 4 * stages)),
         ],
         compiler_params=pltpu.CompilerParams(
-            collective_id=0, has_side_effects=True, vmem_limit_bytes=48 * 1024 * 1024
+            collective_id=0, has_side_effects=True, vmem_limit_bytes=56 * 1024 * 1024
         ),
-    )(vectors, reflectors)
-    projection = nt(current, panels, HIGH)
-    update = pl.pallas_call(
-        functools.partial(solve_kernel, row_count),
-        name="solve",
-        out_shape=jax.ShapeDtypeStruct((rows, count * width), jnp.float32),
-        in_specs=[vmem, vmem, vmem],
-        out_specs=vmem,
-        scratch_shapes=[
-            pltpu.VMEM((2, rows // 2, count * width), jnp.float32),
-            dma((2, 4 * stages)),
-        ],
-        compiler_params=pltpu.CompilerParams(
-            collective_id=1, has_side_effects=True, vmem_limit_bytes=32 * 1024 * 1024
-        ),
-    )(projection, gram, factors)
-    return current - jnp.dot(update, panels, precision=HIGH, preferred_element_type=jnp.float32)
+    )(vectors, reflectors, factors)
+    return current - jnp.dot(update, panels, precision=HIGH, preferred_element_type=single)
 
 
 def solution(mesh):

time: 207 us -> 198 us (0.957)
  matrix products: 16 us -> 9.74 us
    dot_general x2 -> x1, matrix products: 16 us -> 9.74 us  [on_device(): jnp.dot(update, panels, precision=HIGH, preferred_element_type=single)]
    pallas_call x2 -> x1, Pallas kernels: 189 us -> 188 us  [on_device(): pl.pallas_call(functools.partial(kernel, row_count, col_count), name='exc...]
where the time goes in v1:
time: 198 us; the launch traced here: 197 us
  Pallas kernels  188 us (95%)
  matrix products  9.74 us (5%)
    pallas_call x1, Pallas kernels, on_device(): pl.pallas_call(functools.partial(kernel, row_count, col_count), name='exc...  188 us
    dot_general x1, matrix products, on_device(): jnp.dot(update, panels, precision=HIGH, preferred_element_type=single)  9.74 us

profile of v1, /device:TPU:0, one launch (start us, length us, event | category | flops | bytes accessed | tf_op | source)
XLA Modules:
  0.0 197.4 jit_solution(12385740706841665629)
XLA Ops:
  0.0 187.7 %exchange.1 = (f32[512,2048]{1,0:T(8,128)}, f32[768,2048]{1,0:T(8,128)}, f32[512,768]{1,0:T(8,128)}) custom-call(f32[32,32768]{1,0:T(8,128)} %vectors.1, f32[6,64,2048]{2,1,0:T(8,128)} %reflectors.1, f32[6,128,128]{2,1,0:T(8,128)} %factors.1), custom_call_target="tpu_custom_call" | custom-call | tf_op jit(solution)/shard_map/exchange/pallas_call | solution.py:428
  187.7 9.7 %convolution_subtract_fusion = f32[512,2048]{1,0:T(8,128)} fusion(f32[512,2048]{1,0:T(8,128)} %get-tuple-element.8, f32[512,768]{1,0:T(8,128)} %get-tuple-element.9, f32[768,2048]{1,0:T(8,128)} %get-tuple-element.10), kind=kOutput, calls=%fused_computation | convolution fusion | flops 4832886784 | bytes 16252928 | tf_op jit(solution)/shard_map/dot_general | solution.py:465

commit v2 on v1

--- a/solution.py
+++ b/solution.py
@@ -173,7 +173,12 @@
         return target, place
 
     middle = row_count // 2
-    steps = sorted(range(1, row_count), key=lambda step: (abs(step - middle), step))
+    ranked = sorted(range(1, row_count), key=lambda step: (abs(step - middle), step))
+    steps = []
+    while ranked:
+        steps.append(ranked.pop(0))
+        if ranked:
+            steps.append(ranked.pop())
     my_target, my_place = onward(row)
     sends = {}
     for step in steps:
@@ -246,7 +251,7 @@
         def _():
             far.start()
 
-    early = (len(steps) + 1) // 2
+    early = len(steps) // 5
     for step in steps[:early]:
         arrive(step)
     for item in own_panels:

time: 198 us -> 178 us (0.90)
  Pallas kernels: 188 us -> 168 us
    pallas_call x1, Pallas kernels: 188 us -> 168 us  [on_device(): pl.pallas_call(functools.partial(kernel, row_count, col_count), name='exc...]
where the time goes in v2:
time: 178 us
  Pallas kernels  168 us (94%)
  matrix products  9.74 us (5%)
    pallas_call x1, Pallas kernels, on_device(): pl.pallas_call(functools.partial(kernel, row_count, col_count), name='exc...  168 us
    dot_general x1, matrix products, on_device(): jnp.dot(update, panels, precision=HIGH, preferred_element_type=single)  9.74 us

profile of v2, /device:TPU:0, one launch (start us, length us, event | category | flops | bytes accessed | tf_op | source)
XLA Modules:
  0.0 178.1 jit_solution(10904458805690174483)
XLA Ops:
  0.0 168.3 %exchange.1 = (f32[512,2048]{1,0:T(8,128)}, f32[768,2048]{1,0:T(8,128)}, f32[512,768]{1,0:T(8,128)}) custom-call(f32[32,32768]{1,0:T(8,128)} %vectors.1, f32[6,64,2048]{2,1,0:T(8,128)} %reflectors.1, f32[6,128,128]{2,1,0:T(8,128)} %factors.1), custom_call_target="tpu_custom_call" | custom-call | tf_op jit(solution)/shard_map/exchange/pallas_call | solution.py:433
  168.4 9.7 %convolution_subtract_fusion = f32[512,2048]{1,0:T(8,128)} fusion(f32[512,2048]{1,0:T(8,128)} %get-tuple-element.8, f32[512,768]{1,0:T(8,128)} %get-tuple-element.9, f32[768,2048]{1,0:T(8,128)} %get-tuple-element.10), kind=kOutput, calls=%fused_computation | convolution fusion | flops 4832886784 | bytes 16252928 | tf_op jit(solution)/shard_map/dot_general | solution.py:470
